TPU v7x, 32 devices: a whole 2x2x4 slice. The times are simulated.
32 devices in a mesh: dp: 1, tp: 32 (over x, y, z, core).
Axes of the slice: x: 2, y: 2, z: 4, core: 2. Of those that a mesh axis runs over, the one named last changes fastest.
Arguments:
- x: bfloat16 [2048, 7168], P('dp')
- w_gate: bfloat16 [7168, 20480], P(None, 'tp')
- w_up: bfloat16 [7168, 20480], P(None, 'tp')
- w_down: bfloat16 [20480, 7168], P('tp')
Outputs:
- output: bfloat16 [2048, 7168], P('dp')
All inputs are finite; a program needn't handle non-finite values.
Results may differ from a plain program's by a relative error of at most 0.016.
Values are sent between devices in bfloat16 or wider.
A program may use at most 2 GiB of HBM per device.

v0:
```python
import jax
import jax.numpy as jnp
from jax import lax
from jax.sharding import PartitionSpec as P


def solution(mesh):
    def step(x, w_gate, w_up, w_down):
        gate = jnp.dot(x, w_gate, preferred_element_type=jnp.float32)
        up = jnp.dot(x, w_up, preferred_element_type=jnp.float32)
        hidden = (jax.nn.silu(gate) * up).astype(jnp.bfloat16)
        term = jnp.dot(hidden, w_down, preferred_element_type=jnp.float32).astype(jnp.bfloat16)
        return lax.psum(term, "tp")

    return jax.shard_map(
        step,
        mesh=mesh,
        in_specs=(P("dp", None), P(None, "tp"), P(None, "tp"), P("tp", None)),
        out_specs=P("dp", None),
        check_vma=False,
    )
```

profile of v0, /device:TPU:1, one launch (start us, length us, event | category | flops | bytes accessed | tf_op | source)
XLA Modules:
  0.0 564.8 jit_solution(16455374770766841156)
XLA Ops:
  6.5 0.0 all-reduce.2.cloned.1.call-start
  6.5 0.0 copy-start
  6.5 28.3 %fusion = f32[2048,640]{1,0:T(8,128)S(1)} fusion(bf16[2048,7168]{1,0:T(8,128)(2,1)} %param.4, bf16[7168,640]{1,0:T(8,128)(2,1)} %param.5), kind=kOutput, calls=%fused_computation.2 | convolution fusion | flops 18790481920 | bytes 43778048 | tf_op jit(solution)/shard_map/dot_general | solution.py:9
  34.8 0.0 copy-done
  34.8 27.0 %multiply_convert_fusion = bf16[2048,640]{1,0:T(8,128)(2,1)S(1)} fusion(f32[2048,640]{1,0:T(8,128)S(1)} %fusion, bf16[2048,7168]{1,0:T(8,128)(2,1)} %param.4, bf16[7168,640]{1,0:T(8,128)(2,1)S(1)} %copy-done), kind=kOutput, calls=%fused_computation.1 | convolution fusion | flops 18798346240 | bytes 46399488 | tf_op jit(solution)/shard_map/dot_general | solution.py:10
  61.9 30.4 %convolution_convert_fusion = bf16[2048,7168]{1,0:T(8,128)(2,1)} fusion(bf16[2048,640]{1,0:T(8,128)(2,1)S(1)} %multiply_convert_fusion, bf16[640,7168]{1,0:T(8,128)(2,1)} %param.7), kind=kOutput, calls=%fused_computation | convolution fusion | flops 18805161984 | bytes 41156608 | tf_op jit(solution)/shard_map/dot_general | solution.py:12
  92.3 0.0 all-reduce.2.cloned.1.call-update
  92.3 445.5 %all-reduce.2.cloned.1.call-done = bf16[2048,7168]{1,0:T(8,128)(2,1)} async-done(((bf16[2048,7168]{1,0:T(8,128)(2,1)}), bf16[2048,7168]{1,0:T(8,128)(2,1)}) %all-reduce.2.cloned.1.call-update) | async-done | bytes 29360144 | tf_op jit(solution)/shard_map/psum | solution.py:13
  537.8 20.1 %copy.6 = bf16[2048,7168]{1,0:T(8,128)(2,1)} copy(bf16[2048,7168]{1,0:T(8,128)(2,1)} %all-reduce.2.cloned.1.call-done) | data formatting | bytes 58720256
Async XLA Ops:
  6.5 531.2 %all-reduce.2.cloned.1.call-start = ((), (), s32[]{:S(2)}) async-start(), calls=%async_computation | async-start | bytes 58720256 | tf_op jit(solution)/shard_map/psum | solution.py:13
  6.5 28.3 %copy-start = (bf16[7168,640]{1,0:T(8,128)(2,1)S(1)}, bf16[7168,640]{1,0:T(8,128)(2,1)}, u32[]{:S(2)}) copy-start(bf16[7168,640]{1,0:T(8,128)(2,1)} %param.6) | copy-start | bytes 27525124
Sparse Core Ops, SparseCore 0:
  92.4 445.3 all-reduce.1
where the time goes:
time: 566 us; the launch traced here: 565 us
  waiting for transfers between devices  445 us (79%)
  matrix products  85.7 us (15%)
  local copies, waits for them, and re-layouts  20.1 us (4%)
  between operations  13.4 us (2%)
    psum x1, waiting for transfers between devices, step(): return lax.psum(term, 'tp')  445 us
    dot_general x1, matrix products, step(): jnp.dot(hidden, w_down, preferred_element_type=jnp.float32)  30.4 us
    dot_general x1, matrix products, step(): gate = jnp.dot(x, w_gate, preferred_element_type=jnp.float32)  28.3 us
    dot_general x1, matrix products, step(): up = jnp.dot(x, w_up, preferred_element_type=jnp.float32)  27 us
    unnamed x3, local copies, waits for them, and re-layouts  20.1 us
  transfers between devices with their start and end apart: 1, of which 1 were waited for; matrix products, arithmetic and copies ran while one was open for 0% of the time, Pallas kernels for 0%

commit v1 on v0

v1 whole, which is shorter than its diff:
```python
import functools

import jax
import jax.numpy as jnp
from jax import lax
from jax.experimental import pallas as pl
from jax.experimental.pallas import tpu as pltpu
from jax.sharding import PartitionSpec as P

MESH = pl.DeviceIdType.MESH
F32, BF16 = jnp.float32, jnp.bfloat16

ROWS_PER_CHUNK = 128
K_BLOCKS = 4
OFF = (0, 1, 2, 3, 4, 5, 6, 7, 8, 9, 10, 11)
KP = 2 * (OFF[1] - OFF[0])
KX = 2 * (OFF[2] - OFF[1])
KZ1 = 2 * OFF[5] - OFF[2] - OFF[4]
KZ2 = OFF[5] + OFF[4] - 2 * OFF[3]
KZ3 = OFF[5] - OFF[2]
KY = 2 * (OFF[6] - OFF[5])
KT = OFF[1] - OFF[0]
KA = OFF[5] - OFF[1]
KYS = max(2, OFF[6] - OFF[5] + 1)
M1 = 2 * (OFF[7] - OFF[6])
M2 = max(2 * (OFF[8] - OFF[7]), OFF[8] - OFF[6])
M3 = OFF[9] - OFF[6]
MX = 2 * (OFF[10] - OFF[9])
MP = 2 * (OFF[11] - OFF[10])
SEND = 2
GSEND = 4


def kernel(R, x_ref, wg_ref, wu_ref, wd_ref, y_ref, wgu, wdv, xbuf, term, acc, pairsend, pairrecv,
           xsend, xrecv, z1send, z1recv, z2send, z2recv, z3send, z3recv, ysend, yrecv, fin,
           w_sem, x_sem, sp, rp, sx, rx, sz1, rz1, sz2, rz2, sz3, rz3, sy, ry, sl,
           sa1, ra1, sa2, ra2, sa3, ra3, sxa, rxa, spa, rpa):
    N = x_ref.shape[0] // R
    D = x_ref.shape[1]
    F = wg_ref.shape[1]
    W = D // 8
    Q = R // 4
    KB = D // K_BLOCKS

    me = lax.axis_index("tp")
    c = lax.rem(me, 2)
    z = lax.rem(me // 2, 4)
    yy = lax.rem(me // 8, 2)
    xx = me // 16
    odd = lax.rem(z, 2)
    s = z // 2
    is_end = lax.rem(z, 3) == 0
    is_mid = lax.rem(z, 3) != 0
    pair = me + 1 - 2 * c
    xp = me + 16 - 32 * xx
    yp = me + 8 - 16 * yy
    side = me + 2 - 4 * odd
    mid = jnp.where(is_mid, me + 6 - 4 * z, me)
    first = (xp, yp)
    last = (yp, xp)
    f = (xx, yy)

    def quarter(j):
        return pl.multiple_of((j + s * (3 - 2 * j)) * Q, Q)

    def remote(src, dst, ss, rs, dev):
        return pltpu.make_async_remote_copy(
            src_ref=src, dst_ref=dst, send_sem=ss, recv_sem=rs, device_id={"tp": dev}, device_id_type=MESH
        )

    def weight_copies(b):
        rows = pl.ds(b * KB, KB)
        return (
            pltpu.make_async_copy(wg_ref.at[rows], wgu.at[rows, pl.ds(0, F)], w_sem.at[b, 0]),
            pltpu.make_async_copy(wu_ref.at[rows], wgu.at[rows, pl.ds(F, F)], w_sem.at[b, 1]),
        )

    down_copy = pltpu.make_async_copy(wd_ref, wdv, w_sem.at[K_BLOCKS, 0])

    def x_copy(k):
        rows = pl.ds(pl.multiple_of(k * R, R), R)
        return pltpu.make_async_copy(x_ref.at[rows], xbuf.at[lax.rem(k, 2)], x_sem.at[lax.rem(k, 2)])

    x_copy(0).start()
    for b in range(K_BLOCKS):
        for copy in weight_copies(b):
            copy.start()
    down_copy.start()

    barrier = pltpu.get_barrier_semaphore()
    for dev in (pair, xp, yp, side):
        pl.semaphore_signal(barrier, inc=1, device_id={"tp": dev}, device_id_type=MESH)

    @pl.when(is_mid)
    def _():
        pl.semaphore_signal(barrier, inc=1, device_id={"tp": mid}, device_id_type=MESH)
        pl.semaphore_wait(barrier, 5)

    @pl.when(is_end)
    def _():
        pl.semaphore_wait(barrier, 4)

    def c_pair(k):
        a, b = lax.rem(k, SEND), lax.rem(k, KP)
        return remote(pairsend.at[a], pairrecv.at[b], sp.at[a], rp.at[b], pair)

    def c_first(k, t):
        a, b = lax.rem(k, SEND), lax.rem(k, KX)
        return remote(xsend.at[a, t], xrecv.at[b, t], sx.at[t, a], rx.at[t, b], first[t])

    def c_z1(k):
        a, b = lax.rem(k, SEND), lax.rem(k, KZ1)
        return remote(z1send.at[a], z1recv.at[b], sz1.at[a], rz1.at[b], side)

    def c_z2(k):
        a, b = lax.rem(k, SEND), lax.rem(k, KZ2)
        return remote(z2send.at[a], z2recv.at[b], sz2.at[a], rz2.at[b], mid)

    def c_z3(k):
        a, b = lax.rem(k, SEND), lax.rem(k, KZ3)
        return remote(z3send.at[a], z3recv.at[b], sz3.at[a], rz3.at[b], side)

    def c_last(k, t):
        a, b = lax.rem(k, KYS), lax.rem(k, KY)
        return remote(ysend.at[a, t], yrecv.at[b, t], sy.at[t, a], ry.at[t, b], last[t])

    def block(t, flip=False):
        h = 1 - f[t] if flip else f[t]
        return pl.ds(pl.multiple_of((c * 4 + t * 2 + h) * W, 128), W)

    def y_quarter(k, j, t):
        return y_ref.at[pl.ds(pl.multiple_of(k * R + quarter(j), Q), Q), block(t)]

    def y_own(k, t):
        return y_ref.at[pl.ds(pl.multiple_of(k * R + z * Q, Q), Q), block(t)]

    def c_local(k, t):
        a = lax.rem(k, SEND)
        return pltpu.make_async_copy(fin.at[a, t], y_own(k, t), sl.at[t, a])

    def c_a1(k, t, way):
        a, b = lax.rem(k, SEND), lax.rem(k, M1)
        return remote(fin.at[a, t], y_own(k, t), sa1.at[way, t, a], ra1.at[way, t, b], (side, mid)[way])

    def c_a2(k, t, way):
        a, b = lax.rem(k, GSEND), lax.rem(k, M2)
        piece = y_quarter(k, (2, 0)[way], t)
        return remote(piece, piece, sa2.at[way, t, a], ra2.at[t, b], (side, mid)[way])

    def c_a3(k, t):
        a, b = lax.rem(k, GSEND), lax.rem(k, M3)
        piece = y_quarter(k, 3, t)
        return remote(piece, piece, sa3.at[t, a], ra3.at[t, b], side)

    def c_xa(k, t):
        a, b = lax.rem(k, GSEND), lax.rem(k, MX)
        piece = y_ref.at[pl.ds(pl.multiple_of(k * R, R), R), block(t)]
        return remote(piece, piece, sxa.at[t, a], rxa.at[t, b], first[t])

    def c_pa(k):
        a, b = lax.rem(k, GSEND), lax.rem(k, MP)
        piece = y_ref.at[pl.ds(pl.multiple_of(k * R, R), R), pl.ds(pl.multiple_of(c * 4 * W, 128), 4 * W)]
        return remote(piece, piece, spa.at[a], rpa.at[b], pair)

    def s0(k):
        @pl.when(k + 1 < N)
        def _():
            x_copy(k + 1).start()

        x_copy(k).wait()
        xs = lax.rem(k, 2)
        h = None
        for b in range(K_BLOCKS):
            @pl.when(k == 0)
            def _():
                for copy in weight_copies(b):
                    copy.wait()

            part = jnp.dot(xbuf[xs, :, b * KB:(b + 1) * KB], wgu[b * KB:(b + 1) * KB, :], preferred_element_type=F32)
            h = part if h is None else h + part
        hidden = (jax.nn.silu(h[:, :F]) * h[:, F:]).astype(BF16)

        @pl.when(k == 0)
        def _():
            down_copy.wait()

        for t in range(2):
            cols = pl.ds(pl.multiple_of((1 - c) * 4 * W + t * 2 * W, 128), 2 * W)
            part = jnp.dot(hidden, wdv[:, cols], preferred_element_type=F32)
            for i in range(2):
                pairsend[lax.rem(k, SEND), t, i] = part[:, i * W:(i + 1) * W].astype(BF16)
        c_pair(k).start()
        for t in range(2):
            cols = pl.ds(pl.multiple_of(c * 4 * W + t * 2 * W, 128), 2 * W)
            part = jnp.dot(hidden, wdv[:, cols], preferred_element_type=F32)
            for i in range(2):
                term[lax.rem(k, KT), t, i] = part[:, i * W:(i + 1) * W]

    def s1(k):
        c_pair(k).wait_recv()
        a, b, kt, ka = lax.rem(k, SEND), lax.rem(k, KP), lax.rem(k, KT), lax.rem(k, KA)
        for t in range(2):
            h = 1 - f[t]
            xsend[a, t] = (term[kt, t, h] + pairrecv[b, t, h].astype(F32)).astype(BF16)
            c_first(k, t).start()
        for t in range(2):
            h = f[t]
            acc[ka, t] = term[kt, t, h] + pairrecv[b, t, h].astype(F32)

    def s2(k):
        a, b, ka = lax.rem(k, SEND), lax.rem(k, KX), lax.rem(k, KA)
        for t in range(2):
            c_first(k, t).wait_recv()
            acc[ka, t] = acc[ka, t] + xrecv[b, t].astype(F32)

        @pl.when(is_end)
        def _():
            for j in range(1, 4):
                for t in range(2):
                    z1send[a, j - 1, t] = acc[ka, t, pl.ds(quarter(j), Q)].astype(BF16)
            c_z1(k).start()

    def s3(k):
        @pl.when(is_mid)
        def _():
            c_z1(k).wait_recv()
            a, b, ka = lax.rem(k, SEND), lax.rem(k, KZ1), lax.rem(k, KA)
            for j in range(2, 4):
                for t in range(2):
                    z2send[a, j - 2, t] = (
                        acc[ka, t, pl.ds(quarter(j), Q)] + z1recv[b, j - 1, t].astype(F32)
                    ).astype(BF16)
            c_z2(k).start()

    def s4(k):
        @pl.when(is_mid)
        def _():
            c_z2(k).wait_recv()
            a, b, ka = lax.rem(k, SEND), lax.rem(k, KZ2), lax.rem(k, KA)
            for t in range(2):
                z3send[a, t] = (acc[ka, t, pl.ds(quarter(0), Q)] + z2recv[b, 1, t].astype(F32)).astype(BF16)
            c_z3(k).start()

    def s5(k):
        a, ka = lax.rem(k, KYS), lax.rem(k, KA)

        @pl.when(is_mid)
        def _():
            b1, b2 = lax.rem(k, KZ1), lax.rem(k, KZ2)
            for t in range(2):
                ysend[a, t] = (
                    acc[ka, t, pl.ds(quarter(1), Q)] + z1recv[b1, 0, t].astype(F32) + z2recv[b2, 0, t].astype(F32)
                ).astype(BF16)

        @pl.when(is_end)
        def _():
            c_z3(k).wait_recv()
            b3 = lax.rem(k, KZ3)
            for t in range(2):
                ysend[a, t] = (acc[ka, t, pl.ds(quarter(0), Q)] + z3recv[b3, t].astype(F32)).astype(BF16)

        for t in range(2):
            c_last(k, t).start()

    def s6(k):
        a, b, g = lax.rem(k, KYS), lax.rem(k, KY), lax.rem(k, SEND)
        for t in range(2):
            c_last(k, t).wait_recv()
            fin[g, t] = (ysend[a, t].astype(F32) + yrecv[b, t].astype(F32)).astype(BF16)
        for t in range(2):
            c_local(k, t).start()
            c_a1(k, t, 0).start()

        @pl.when(is_mid)
        def _():
            for t in range(2):
                c_a1(k, t, 1).start()

    def s7(k):
        for t in range(2):
            c_a1(k, t, 0).wait_recv()

        @pl.when(is_mid)
        def _():
            for t in range(2):
                c_a2(k, t, 1).start()
            for t in range(2):
                c_a1(k, t, 1).wait_recv()
                c_a2(k, t, 0).start()

    def s8(k):
        for t in range(2):
            c_a2(k, t, 0).wait_recv()

        @pl.when(is_mid)
        def _():
            for t in range(2):
                c_a3(k, t).start()

    def s9(k):
        @pl.when(is_end)
        def _():
            for t in range(2):
                c_a3(k, t).wait_recv()

        for t in range(2):
            c_xa(k, t).start()

    def s10(k):
        for t in range(2):
            c_xa(k, t).wait_recv()
        c_pa(k).start()

    def s11(k):
        c_pa(k).wait_recv()

    def d0(k):
        c_pair(k).wait_send()

    def d1(k):
        for t in range(2):
            c_first(k, t).wait_send()

    def d2(k):
        @pl.when(is_end)
        def _():
            c_z1(k).wait_send()

    def d3(k):
        @pl.when(is_mid)
        def _():
            c_z2(k).wait_send()

    def d4(k):
        @pl.when(is_mid)
        def _():
            c_z3(k).wait_send()

    def d5(k):
        for t in range(2):
            c_last(k, t).wait_send()

    def d6(k):
        for t in range(2):
            c_local(k, t).wait()
            c_a1(k, t, 0).wait_send()

        @pl.when(is_mid)
        def _():
            for t in range(2):
                c_a1(k, t, 1).wait_send()

    def d7(k):
        @pl.when(is_mid)
        def _():
            for t in range(2):
                c_a2(k, t, 1).wait_send()
                c_a2(k, t, 0).wait_send()

    def d8(k):
        @pl.when(is_mid)
        def _():
            for t in range(2):
                c_a3(k, t).wait_send()

    def d9(k):
        for t in range(2):
            c_xa(k, t).wait_send()

    def d10(k):
        c_pa(k).wait_send()

    stages = (
        (s0, d0, SEND), (s1, d1, SEND), (s2, d2, SEND), (s3, d3, SEND), (s4, d4, SEND), (s5, d5, KYS),
        (s6, d6, SEND), (s7, d7, GSEND), (s8, d8, GSEND), (s9, d9, GSEND), (s10, d10, GSEND), (s11, None, 0),
    )
    ticks = N + max(off + lag for off, (_, _, lag) in zip(OFF, stages))

    def tick(i, carry):
        for off, (run, drain, lag) in reversed(tuple(zip(OFF, stages))):
            if drain is not None:
                k_old = i - off - lag

                @pl.when((k_old >= 0) & (k_old < N))
                def _():
                    drain(k_old)

            k = i - off

            @pl.when((k >= 0) & (k < N))
            def _():
                run(k)

        return carry

    lax.fori_loop(0, ticks, tick, 0)


def solution(mesh):
    def step(x, w_gate, w_up, w_down):
        rows, D = x.shape
        F = w_gate.shape[1]
        R = min(ROWS_PER_CHUNK, rows // 8)
        W, Q = D // 8, R // 4
        any_spec = pl.BlockSpec(memory_space=pl.ANY)
        dma = lambda *shape: pltpu.SemaphoreType.DMA(shape)
        return pl.pallas_call(
            functools.partial(kernel, R),
            out_shape=jax.ShapeDtypeStruct((rows, D), BF16),
            in_specs=[any_spec] * 4,
            out_specs=any_spec,
            scratch_shapes=[
                pltpu.VMEM((D, 2 * F), BF16),
                pltpu.VMEM((F, D), BF16),
                pltpu.VMEM((2, R, D), BF16),
                pltpu.VMEM((KT, 2, 2, R, W), F32),
                pltpu.VMEM((KA, 2, R, W), F32),
                pltpu.VMEM((SEND, 2, 2, R, W), BF16),
                pltpu.VMEM((KP, 2, 2, R, W), BF16),
                pltpu.VMEM((SEND, 2, R, W), BF16),
                pltpu.VMEM((KX, 2, R, W), BF16),
                pltpu.VMEM((SEND, 3, 2, Q, W), BF16),
                pltpu.VMEM((KZ1, 3, 2, Q, W), BF16),
                pltpu.VMEM((SEND, 2, 2, Q, W), BF16),
                pltpu.VMEM((KZ2, 2, 2, Q, W), BF16),
                pltpu.VMEM((SEND, 2, Q, W), BF16),
                pltpu.VMEM((KZ3, 2, Q, W), BF16),
                pltpu.VMEM((KYS, 2, Q, W), BF16),
                pltpu.VMEM((KY, 2, Q, W), BF16),
                pltpu.VMEM((SEND, 2, Q, W), BF16),
                dma(K_BLOCKS + 1, 2), dma(2),
                dma(SEND), dma(KP),
                dma(2, SEND), dma(2, KX),
                dma(SEND), dma(KZ1),
                dma(SEND), dma(KZ2),
                dma(SEND), dma(KZ3),
                dma(2, KYS), dma(2, KY),
                dma(2, SEND),
                dma(2, 2, SEND), dma(2, 2, M1),
                dma(2, 2, GSEND), dma(2, M2),
                dma(2, GSEND), dma(2, M3),
                dma(2, GSEND), dma(2, MX),
                dma(GSEND), dma(MP),
            ],
            compiler_params=pltpu.CompilerParams(
                collective_id=0, has_side_effects=True, vmem_limit_bytes=67043328
            ),
            name="mlp_all_reduce",
        )(x, w_gate, w_up, w_down)

    return jax.shard_map(
        step,
        mesh=mesh,
        in_specs=(P("dp", None), P(None, "tp"), P(None, "tp"), P("tp", None)),
        out_specs=P("dp", None),
        check_vma=False,
    )
```

time: 566 us -> 252 us (0.45)
  waiting for transfers between devices: 445 us -> 0 us
  Pallas kernels: 0 us -> 232 us
  matrix products: 85.7 us -> 0 us
  between operations: 13.4 us -> 0.01 us
    psum x1 -> x0, waiting for transfers between devices: 445 us -> none  [step(): return lax.psum(term, 'tp')]
    pallas_call x0 -> x1, Pallas kernels: none -> 232 us  [step(): pl.pallas_call(functools.partial(kernel, R), out_shape=jax.ShapeDtypeStru...]
    dot_general x3 -> x0, matrix products: 85.7 us -> none  [the longest x1 30.4 us: step(): jnp.dot(hidden, w_down, preferred_element_type=jnp.float32)]
    unnamed x3 -> x1, local copies, waits for them, and re-layouts: 20.1 us -> 20.2 us
  transfers between devices with their start and end apart: 1 -> 0, of which waited for: 1 -> 0; matrix products, arithmetic and copies ran while one was open for 0% -> 0% of each run, Pallas kernels for 0% -> 0%
where the time goes in v1:
time: 252 us
  Pallas kernels  232 us (92%)
  local copies, waits for them, and re-layouts  20.2 us (8%)
    pallas_call x1, Pallas kernels, step(): pl.pallas_call(functools.partial(kernel, R), out_shape=jax.ShapeDtypeStru...  232 us
    unnamed x1, local copies, waits for them, and re-layouts  20.2 us

profile of v1, /device:TPU:1, one launch (start us, length us, event | category | flops | bytes accessed | tf_op | source)
XLA Modules:
  0.0 252.2 jit_solution(16033609138314882187)
XLA Ops:
  0.0 232.0 %mlp_all_reduce.1 = bf16[2048,7168]{1,0:T(8,128)(2,1)} custom-call(bf16[2048,7168]{1,0:T(8,128)(2,1)} %x_ref.1, bf16[7168,640]{1,0:T(8,128)(2,1)} %wg_ref.1, bf16[7168,640]{1,0:T(8,128)(2,1)} %wu_ref.1, bf16[640,7168]{1,0:T(8,128)(2,1)} %wd_ref.1), custom_call_target="tpu_custom_call" | custom-call | tf_op jit(solution)/shard_map/mlp_all_reduce/pallas_call | solution.py:407
  232.0 20.2 %copy.6 = bf16[2048,7168]{1,0:T(8,128)(2,1)} copy(bf16[2048,7168]{1,0:T(8,128)(2,1)} %mlp_all_reduce.1) | data formatting | bytes 58720256

commit v2 on v1

v2 whole, which is shorter than its diff:
```python
import functools

import jax
import jax.numpy as jnp
from jax import lax
from jax.experimental import pallas as pl
from jax.experimental.pallas import tpu as pltpu
from jax.sharding import PartitionSpec as P

MESH = pl.DeviceIdType.MESH
F32, BF16 = jnp.float32, jnp.bfloat16

ROWS_PER_CHUNK = 128
PIECES = 2
TAIL = 2
OFF = (0, 1, 3, 4, 5, 6, 7)
GOFF = (0, 2, 4, 6, 8, 10)
KP = 2 * (OFF[1] - OFF[0])
KX = 2 * (OFF[2] - OFF[1])
KZ1 = OFF[5] - OFF[2]
KZ2 = 2 * (OFF[4] - OFF[3])
KZ3 = OFF[5] - OFF[2]
KY = 2 * (OFF[6] - OFF[5])
KT = OFF[1] - OFF[0]
KO = OFF[5] - OFF[1]
KI = OFF[3] - OFF[1]
SEND = 3
PSEND = 2
KC1 = OFF[4] - OFF[1]
KC2 = 2 * (OFF[3] - OFF[2])
KC3 = OFF[5] - OFF[1]
KC4 = 2 * (OFF[5] - OFF[4])
KYS = max(SEND, OFF[6] - OFF[5] + 1)
M1 = GOFF[3] - GOFF[0]
M2 = 2 * (GOFF[2] - GOFF[1])
M3 = GOFF[3] - GOFF[0]
MO = 2 * GOFF[4] - GOFF[0] - GOFF[2]
MI = 2 * (GOFF[4] - GOFF[2])
MP = 2 * (GOFF[5] - GOFF[4])
GSEND = 6


def split(W):
    return W * 5 // 7 // 128 * 128 if W > 256 else W // 2


def kernel(R, x_ref, wg_ref, wu_ref, wd_ref, y_ref, xbuf, hidden, term, acco, acci, pairsend, pairrecv,
           xsend, xrecv, z1send, z1recv, z2send, z2recv, z3send, z3recv, ysend, yrecv, fin,
           accco, accci, c1send, c1recv, c2send, c2recv, c3send, c3recv, c4send, c4recv,
           w_sem, x_sem, sp, rp, sx, rx, sz1, rz1, sz2, rz2, sz3, rz3, sy, ry,
           sc1, rc1, sc2, rc2, sc3, rc3, sc4, rc4, ready,
           sa1, ra1, sa2, ra2, sa3, ra3, sxo, rxo, sxi, rxi, spa, rpa):
    N = x_ref.shape[0] // R
    D = x_ref.shape[1]
    F = wg_ref.shape[1]
    W = D // 8
    W1 = split(W)
    Q = R // 2
    G = Q // PIECES
    NG = N * PIECES
    KB = y_ref.shape[0] - F
    NB = D // KB
    REST = D - NB * KB
    assert 2 * REST <= KB and NB * 2 * F + F <= D

    me = lax.axis_index("tp")
    c = lax.rem(me, 2)
    z = lax.rem(me // 2, 4)
    yy = lax.rem(me // 8, 2)
    xx = me // 16
    odd = lax.rem(z, 2)
    s = z // 2
    is_end = lax.rem(z, 3) == 0
    is_mid = lax.rem(z, 3) != 0
    pair = me + 1 - 2 * c
    xp = me + 16 - 32 * xx
    yp = me + 8 - 16 * yy
    side = me + 2 - 4 * odd
    mid = jnp.where(is_mid, me + 6 - 4 * z, me)
    first = (xp, yp)
    last = (yp, xp)
    f = (xx, yy)

    out_rows = pl.multiple_of((1 - s) * Q, Q)
    in_rows = pl.multiple_of(s * Q, Q)

    def remote(src, dst, ss, rs, dev):
        return pltpu.make_async_remote_copy(
            src_ref=src, dst_ref=dst, send_sem=ss, recv_sem=rs, device_id={"tp": dev}, device_id_type=MESH
        )

    def weight_copies(b):
        copies = []
        for i, ref in enumerate((wg_ref, wu_ref)):
            if b < NB:
                dst = y_ref.at[pl.ds(F, KB), pl.ds((2 * b + i) * F, F)]
                src = ref.at[pl.ds(b * KB, KB)]
            else:
                dst = y_ref.at[pl.ds(F + i * REST, REST), pl.ds(NB * 2 * F, F)]
                src = ref.at[pl.ds(NB * KB, REST)]
            copies.append(pltpu.make_async_copy(src, dst, w_sem.at[b, i]))
        return copies

    down_copy = pltpu.make_async_copy(wd_ref, y_ref.at[pl.ds(0, F)], w_sem.at[NB + 1, 0])

    def x_copy(k):
        rows = pl.ds(pl.multiple_of(k * R, R), R)
        return pltpu.make_async_copy(x_ref.at[rows], xbuf.at[lax.rem(k, 2)], x_sem.at[lax.rem(k, 2)])

    x_copy(0).start()
    for b in range(NB + 1):
        for copy in weight_copies(b):
            copy.start()
    down_copy.start()

    barrier = pltpu.get_barrier_semaphore()
    for dev in (pair, xp, yp, side):
        pl.semaphore_signal(barrier, inc=1, device_id={"tp": dev}, device_id_type=MESH)

    @pl.when(is_mid)
    def _():
        pl.semaphore_signal(barrier, inc=1, device_id={"tp": mid}, device_id_type=MESH)
        pl.semaphore_wait(barrier, 5)

    @pl.when(is_end)
    def _():
        pl.semaphore_wait(barrier, 4)

    def c_pair(k):
        a, b = lax.rem(k, PSEND), lax.rem(k, KP)
        return remote(pairsend.at[a], pairrecv.at[b], sp.at[a], rp.at[b], pair)

    def c_first(k, t):
        a, b = lax.rem(k, SEND), lax.rem(k, KX)
        return remote(xsend.at[a, t], xrecv.at[b, t], sx.at[t, a], rx.at[t, b], first[t])

    def c_z1(k):
        a, b = lax.rem(k, SEND), lax.rem(k, KZ1)
        return remote(z1send.at[a], z1recv.at[b], sz1.at[a], rz1.at[b], side)

    def c_z2(k):
        a, b = lax.rem(k, SEND), lax.rem(k, KZ2)
        return remote(z2send.at[a], z2recv.at[b], sz2.at[a], rz2.at[b], mid)

    def c_z3(k):
        a, b = lax.rem(k, SEND), lax.rem(k, KZ3)
        return remote(z3send.at[a], z3recv.at[b], sz3.at[a], rz3.at[b], side)

    def c_last(k, t):
        a, b = lax.rem(k, KYS), lax.rem(k, KY)
        return remote(ysend.at[a, t], yrecv.at[b, t], sy.at[t, a], ry.at[t, b], last[t])

    def c_c1(k):
        a, b = lax.rem(k, SEND), lax.rem(k, KC1)
        return remote(c1send.at[a], c1recv.at[b], sc1.at[a], rc1.at[b], side)

    def c_c2(k):
        a, b = lax.rem(k, SEND), lax.rem(k, KC2)
        return remote(c2send.at[a], c2recv.at[b], sc2.at[a], rc2.at[b], mid)

    def c_c3(k):
        a, b = lax.rem(k, SEND), lax.rem(k, KC3)
        return remote(c3send.at[a], c3recv.at[b], sc3.at[a], rc3.at[b], side)

    def c_c4(k, t):
        a, b = lax.rem(k, SEND), lax.rem(k, KC4)
        return remote(c4send.at[a, t], c4recv.at[b, t], sc4.at[t, a], rc4.at[t, b], first[t])

    def block(t, flip=False):
        h = 1 - f[t] if flip else f[t]
        return pl.ds(pl.multiple_of((c * 4 + t * 2 + h) * W, 128), W)

    def y_piece(p, at, t):
        row = (p // PIECES) * R + at + lax.rem(p, PIECES) * G
        return y_ref.at[pl.ds(pl.multiple_of(row, G), G), block(t)]

    def fin_piece(p, t):
        return fin.at[p // PIECES, t, pl.ds(pl.multiple_of(lax.rem(p, PIECES) * G, G), G)]

    def c_a1(p, t):
        a, b = lax.rem(p, GSEND), lax.rem(p, M1)
        return remote(fin_piece(p, t), y_piece(p, out_rows, t), sa1.at[t, a], ra1.at[t, b], side)

    def c_a2(p, t):
        a, b = lax.rem(p, GSEND), lax.rem(p, M2)
        piece = y_piece(p, out_rows, t)
        return remote(piece, piece, sa2.at[t, a], ra2.at[t, b], mid)

    def c_a3(p, t):
        a, b = lax.rem(p, GSEND), lax.rem(p, M3)
        piece = y_piece(p, in_rows, t)
        return remote(piece, piece, sa3.at[t, a], ra3.at[t, b], side)

    def c_xo(p, t, src=None):
        a, b = lax.rem(p, GSEND), lax.rem(p, MO)
        piece = y_piece(p, out_rows, t)
        return remote(piece if src is None else src, piece, sxo.at[t, a], rxo.at[t, b], first[t])

    def c_xi(p, t):
        a, b = lax.rem(p, GSEND), lax.rem(p, MI)
        piece = y_piece(p, in_rows, t)
        return remote(piece, piece, sxi.at[t, a], rxi.at[t, b], first[t])

    def c_pa(p, h):
        a, b = lax.rem(p, GSEND), lax.rem(p, MP)
        row = (p // PIECES) * R + h * Q + lax.rem(p, PIECES) * G
        piece = y_ref.at[pl.ds(pl.multiple_of(row, G), G), pl.ds(pl.multiple_of(c * 4 * W, 128), 4 * W)]
        return remote(piece, piece, spa.at[h, a], rpa.at[h, b], pair)

    def h0(k):
        @pl.when(k + 1 < N)
        def _():
            x_copy(k + 1).start()

        x_copy(k).wait()
        xs = lax.rem(k, 2)
        h = None
        for b in range(NB + 1):
            @pl.when(k == 0)
            def _():
                for copy in weight_copies(b):
                    copy.wait()

            if b < NB:
                part = jnp.dot(
                    xbuf[xs, :, b * KB:(b + 1) * KB],
                    y_ref[F:F + KB, b * 2 * F:(b + 1) * 2 * F],
                    preferred_element_type=F32,
                )
                h = part if h is None else h + part
        gate, up = (
            h[:, i * F:(i + 1) * F] + jnp.dot(
                xbuf[xs, :, NB * KB:],
                y_ref[F + i * REST:F + (i + 1) * REST, NB * 2 * F:NB * 2 * F + F],
                preferred_element_type=F32,
            )
            for i in range(2)
        )
        hidden[...] = (jax.nn.silu(gate) * up).astype(BF16)

    def s0(k):
        @pl.when(k == 0)
        def _():
            down_copy.wait()

        for t in range(2):
            cols = pl.ds(pl.multiple_of((1 - c) * 4 * W + t * 2 * W, 128), 2 * W)
            part = jnp.dot(hidden[...], y_ref[:F, cols], preferred_element_type=F32)
            for i in range(2):
                pairsend[lax.rem(k, PSEND), t, i] = part[:, i * W:(i + 1) * W].astype(BF16)
        c_pair(k).start()
        for t in range(2):
            cols = pl.ds(pl.multiple_of(c * 4 * W + t * 2 * W, 128), 2 * W)
            part = jnp.dot(hidden[...], y_ref[:F, cols], preferred_element_type=F32)
            for i in range(2):
                term[lax.rem(k, KT), t, i] = part[:, i * W:(i + 1) * W]

        @pl.when(k == N - 1)
        def _():
            for dev in (pair, xp, yp, side):
                pl.semaphore_signal(ready, inc=1, device_id={"tp": dev}, device_id_type=MESH)

            @pl.when(is_mid)
            def _():
                pl.semaphore_signal(ready, inc=1, device_id={"tp": mid}, device_id_type=MESH)

    def s1(k):
        c_pair(k).wait_recv()
        a, b, kt = lax.rem(k, SEND), lax.rem(k, KP), lax.rem(k, KT)
        ki, ko = lax.rem(k, KI), lax.rem(k, KO)
        for t in range(2):
            h = 1 - f[t]
            xsend[a, t] = (term[kt, t, h, :, :W1] + pairrecv[b, t, h, :, :W1].astype(F32)).astype(BF16)
            c_first(k, t).start()
        for t in range(2):
            for h in range(2):
                for dst, slot, at in ((accci, ki, in_rows), (accco, ko, out_rows)):
                    rows = pl.ds(at, Q)
                    dst[slot, t, h] = term[kt, t, h, rows, W1:] + pairrecv[b, t, h, rows, W1:].astype(F32)

        @pl.when(is_end)
        def _():
            c1send[a] = accci[ki].astype(BF16)
            c_c1(k).start()

        for t in range(2):
            h = f[t]
            for dst, slot, at in ((acci, ki, in_rows), (acco, ko, out_rows)):
                rows = pl.ds(at, Q)
                dst[slot, t] = term[kt, t, h, rows, :W1] + pairrecv[b, t, h, rows, :W1].astype(F32)

    def s2(k):
        a, b, ki, ko = lax.rem(k, SEND), lax.rem(k, KX), lax.rem(k, KI), lax.rem(k, KO)

        @pl.when(is_mid)
        def _():
            c_c1(k).wait_recv()
            c2send[a] = (accci[ki] + c1recv[lax.rem(k, KC1)].astype(F32)).astype(BF16)
            c_c2(k).start()

        for t in range(2):
            c_first(k, t).wait_recv()
            acci[ki, t] = acci[ki, t] + xrecv[b, t, pl.ds(in_rows, Q)].astype(F32)
            acco[ko, t] = acco[ko, t] + xrecv[b, t, pl.ds(out_rows, Q)].astype(F32)

        @pl.when(is_end)
        def _():
            z1send[a] = acci[ki].astype(BF16)
            c_z1(k).start()

    def s3(k):
        @pl.when(is_mid)
        def _():
            a, b, ki, ko = lax.rem(k, SEND), lax.rem(k, KZ1), lax.rem(k, KI), lax.rem(k, KO)
            c_c2(k).wait_recv()
            c3send[a] = (accco[ko] + c2recv[lax.rem(k, KC2)].astype(F32)).astype(BF16)
            c_c3(k).start()
            c_z1(k).wait_recv()
            z2send[a] = (acci[ki] + z1recv[b].astype(F32)).astype(BF16)
            c_z2(k).start()

    def s4(k):
        a, b, ko = lax.rem(k, SEND), lax.rem(k, KZ2), lax.rem(k, KO)

        @pl.when(is_end)
        def _():
            c_c3(k).wait_recv()
            for t in range(2):
                h = 1 - f[t]
                c4send[a, t] = (accco[ko, t, h] + c3recv[lax.rem(k, KC3), t, h].astype(F32)).astype(BF16)
                c_c4(k, t).start()

        @pl.when(is_mid)
        def _():
            c_z2(k).wait_recv()
            z3send[a] = (acco[ko] + z2recv[b].astype(F32)).astype(BF16)
            c_z3(k).start()

    def s5(k):
        @pl.when(is_end)
        def _():
            a, b, ko = lax.rem(k, KYS), lax.rem(k, KZ3), lax.rem(k, KO)
            for t in range(2):
                h = f[t]
                c_c4(k, t).wait_recv()
                ysend[a, t, :, W1:] = (
                    accco[ko, t, h]
                    + c3recv[lax.rem(k, KC3), t, h].astype(F32)
                    + c4recv[lax.rem(k, KC4), t].astype(F32)
                ).astype(BF16)
            c_z3(k).wait_recv()
            for t in range(2):
                ysend[a, t, :, :W1] = (acco[ko, t] + z3recv[b, t].astype(F32)).astype(BF16)
                c_last(k, t).start()

    def s6(k):
        @pl.when(is_end)
        def _():
            a, b = lax.rem(k, KYS), lax.rem(k, KY)
            for t in range(2):
                c_last(k, t).wait_recv()
                fin[k, t] = (ysend[a, t].astype(F32) + yrecv[b, t].astype(F32)).astype(BF16)

    def open_gather():
        @pl.when(is_mid)
        def _():
            pl.semaphore_wait(ready, 5)

        @pl.when(is_end)
        def _():
            pl.semaphore_wait(ready, 4)

    def g0(p):
        @pl.when(is_end)
        def _():
            for t in range(2):
                c_a1(p, t).start()
                c_xo(p, t, fin_piece(p, t)).start()
            for t in range(2):
                y_piece(p, out_rows, t)[...] = fin_piece(p, t)[...]

    def g1(p):
        @pl.when(is_mid)
        def _():
            for t in range(2):
                c_a1(p, t).wait_recv()
                c_a2(p, t).start()
                c_xo(p, t).start()

    def g2(p):
        @pl.when(is_mid)
        def _():
            for t in range(2):
                c_a2(p, t).wait_recv()
                c_a3(p, t).start()
                c_xi(p, t).start()

    def g3(p):
        @pl.when(is_end)
        def _():
            for t in range(2):
                c_a3(p, t).wait_recv()
                c_xi(p, t).start()

    def g4(p):
        for t in range(2):
            c_xo(p, t).wait_recv()
            c_xi(p, t).wait_recv()
        for h in range(2):
            c_pa(p, h).start()

    def g5(p):
        for h in range(2):
            c_pa(p, h).wait_recv()

    def d0(k):
        c_pair(k).wait_send()

    def d1(k):
        for t in range(2):
            c_first(k, t).wait_send()

        @pl.when(is_end)
        def _():
            c_c1(k).wait_send()

    def d2(k):
        @pl.when(is_end)
        def _():
            c_z1(k).wait_send()

        @pl.when(is_mid)
        def _():
            c_c2(k).wait_send()

    def d3(k):
        @pl.when(is_mid)
        def _():
            c_c3(k).wait_send()
            c_z2(k).wait_send()

    def d4(k):
        @pl.when(is_end)
        def _():
            for t in range(2):
                c_c4(k, t).wait_send()

        @pl.when(is_mid)
        def _():
            c_z3(k).wait_send()

    def d5(k):
        @pl.when(is_end)
        def _():
            for t in range(2):
                c_last(k, t).wait_send()

    def e0(p):
        @pl.when(is_end)
        def _():
            for t in range(2):
                c_a1(p, t).wait_send()
                c_xo(p, t, fin_piece(p, t)).wait_send()

    def e1(p):
        @pl.when(is_mid)
        def _():
            for t in range(2):
                c_a2(p, t).wait_send()
                c_xo(p, t).wait_send()

    def e2(p):
        @pl.when(is_mid)
        def _():
            for t in range(2):
                c_a3(p, t).wait_send()
                c_xi(p, t).wait_send()

    def e3(p):
        @pl.when(is_end)
        def _():
            for t in range(2):
                c_xi(p, t).wait_send()

    def e4(p):
        for h in range(2):
            c_pa(p, h).wait_send()

    reduce_stages = (
        (s0, d0, PSEND), (s1, d1, SEND), (h0, None, 0), (s2, d2, SEND), (s3, d3, SEND), (s4, d4, SEND), (s5, d5, KYS),
        (s6, None, 0),
    )
    gather_stages = (
        (g0, e0, GSEND), (g1, e1, GSEND), (g2, e2, GSEND), (g3, e3, GSEND), (g4, e4, GSEND), (g5, None, 0),
    )

    def advance(i, count, offsets, stages):
        for off, (run, drain, lag) in reversed(tuple(zip(offsets, stages))):
            if drain is not None:
                k_old = i - off - lag

                @pl.when((k_old >= 0) & (k_old < count))
                def _():
                    drain(k_old)

            if run is not None:
                k = i - off

                @pl.when((k >= 0) & (k < count))
                def _():
                    run(k)

    offsets = OFF[:2] + OFF[:1] + OFF[2:]
    tail_stages = ((None, d0, PSEND), reduce_stages[1], (None, None, 0)) + reduce_stages[3:]

    def reduce_tick(i, carry):
        advance(i, N, offsets, reduce_stages)
        return carry

    def gather_tick(u, carry):
        @pl.when(lax.rem(u, TAIL) == 0)
        def _():
            advance(N + u // TAIL, N, offsets, tail_stages)

        advance(u, NG, GOFF, gather_stages)
        return carry

    lax.fori_loop(0, N, reduce_tick, 0)
    open_gather()
    ticks = NG + max(off + lag for off, (_, _, lag) in zip(GOFF, gather_stages))
    lax.fori_loop(0, ticks, gather_tick, 0)


def store_kernel(y_ref, o_ref, sem):
    blocks = sem.shape[0]
    rows = y_ref.shape[0] // blocks
    copies = [
        pltpu.make_async_copy(y_ref.at[pl.ds(i * rows, rows)], o_ref.at[pl.ds(i * rows, rows)], sem.at[i])
        for i in range(blocks)
    ]
    for copy in copies:
        copy.start()
    for copy in copies:
        copy.wait()


def solution(mesh):
    def step(x, w_gate, w_up, w_down):
        rows, D = x.shape
        F = w_gate.shape[1]
        R = min(ROWS_PER_CHUNK, rows // 8)
        W, Q = D // 8, R // 2
        W1 = split(W)
        W3 = W - W1
        any_spec = pl.BlockSpec(memory_space=pl.ANY)
        dma = lambda *shape: pltpu.SemaphoreType.DMA(shape)
        blocks = D // (rows - F) + 2
        y = pl.pallas_call(
            functools.partial(kernel, R),
            out_shape=pltpu.VMEM((rows, D), BF16),
            in_specs=[any_spec] * 4,
            out_specs=pl.BlockSpec(memory_space=pltpu.VMEM),
            scratch_shapes=[
                pltpu.VMEM((2, R, D), BF16),
                pltpu.VMEM((R, F), BF16),
                pltpu.VMEM((KT, 2, 2, R, W), F32),
                pltpu.VMEM((KO, 2, Q, W1), F32),
                pltpu.VMEM((KI, 2, Q, W1), F32),
                pltpu.VMEM((PSEND, 2, 2, R, W), BF16),
                pltpu.VMEM((KP, 2, 2, R, W), BF16),
                pltpu.VMEM((SEND, 2, R, W1), BF16),
                pltpu.VMEM((KX, 2, R, W1), BF16),
                pltpu.VMEM((SEND, 2, Q, W1), BF16),
                pltpu.VMEM((KZ1, 2, Q, W1), BF16),
                pltpu.VMEM((SEND, 2, Q, W1), BF16),
                pltpu.VMEM((KZ2, 2, Q, W1), BF16),
                pltpu.VMEM((SEND, 2, Q, W1), BF16),
                pltpu.VMEM((KZ3, 2, Q, W1), BF16),
                pltpu.VMEM((KYS, 2, Q, W), BF16),
                pltpu.VMEM((KY, 2, Q, W), BF16),
                pltpu.VMEM((rows // R, 2, Q, W), BF16),
                pltpu.VMEM((KO, 2, 2, Q, W3), F32),
                pltpu.VMEM((KI, 2, 2, Q, W3), F32),
                pltpu.VMEM((SEND, 2, 2, Q, W3), BF16),
                pltpu.VMEM((KC1, 2, 2, Q, W3), BF16),
                pltpu.VMEM((SEND, 2, 2, Q, W3), BF16),
                pltpu.VMEM((KC2, 2, 2, Q, W3), BF16),
                pltpu.VMEM((SEND, 2, 2, Q, W3), BF16),
                pltpu.VMEM((KC3, 2, 2, Q, W3), BF16),
                pltpu.VMEM((SEND, 2, Q, W3), BF16),
                pltpu.VMEM((KC4, 2, Q, W3), BF16),
                dma(blocks, 2), dma(2),
                dma(PSEND), dma(KP),
                dma(2, SEND), dma(2, KX),
                dma(SEND), dma(KZ1),
                dma(SEND), dma(KZ2),
                dma(SEND), dma(KZ3),
                dma(2, KYS), dma(2, KY),
                dma(SEND), dma(KC1),
                dma(SEND), dma(KC2),
                dma(SEND), dma(KC3),
                dma(2, SEND), dma(2, KC4),
                pltpu.SemaphoreType.REGULAR,
                dma(2, GSEND), dma(2, M1),
                dma(2, GSEND), dma(2, M2),
                dma(2, GSEND), dma(2, M3),
                dma(2, GSEND), dma(2, MO),
                dma(2, GSEND), dma(2, MI),
                dma(2, GSEND), dma(2, MP),
            ],
            compiler_params=pltpu.CompilerParams(
                collective_id=0, has_side_effects=True, vmem_limit_bytes=35 * 2**20
            ),
            name="mlp_all_reduce",
        )(x, w_gate, w_up, w_down)
        return pl.pallas_call(
            store_kernel,
            out_shape=jax.ShapeDtypeStruct((rows, D), BF16),
            in_specs=[any_spec],
            out_specs=any_spec,
            scratch_shapes=[dma(8)],
            compiler_params=pltpu.CompilerParams(vmem_limit_bytes=2**20),
            name="store",
        )(y)

    return jax.shard_map(
        step,
        mesh=mesh,
        in_specs=(P("dp", None), P(None, "tp"), P(None, "tp"), P("tp", None)),
        out_specs=P("dp", None),
        check_vma=False,
    )
```

time: 252 us -> 243 us (0.964)
  local copies, waits for them, and re-layouts: 20.2 us -> 0 us
  Pallas kernels: 232 us -> 243 us
    unnamed x1 -> x0, local copies, waits for them, and re-layouts: 20.2 us -> none
    pallas_call x1 -> x2, Pallas kernels: 232 us -> 243 us  [the longest x1 233 us: step(): pl.pallas_call(functools.partial(kernel, R), out_shape=pltpu.VMEM((rows,...]
where the time goes in v2:
time: 243 us
  Pallas kernels  243 us (100%)
    pallas_call x1, Pallas kernels, step(): pl.pallas_call(functools.partial(kernel, R), out_shape=pltpu.VMEM((rows,...  233 us
    pallas_call x1, Pallas kernels, step(): pl.pallas_call(store_kernel, out_shape=jax.ShapeDtypeStruct((rows, D), BF...  9.84 us

profile of v2, /device:TPU:1, one launch (start us, length us, event | category | flops | bytes accessed | tf_op | source)
XLA Modules:
  0.0 242.6 jit_solution(17780297068047201149)
XLA Ops:
  0.0 232.8 %mlp_all_reduce.1.y_ref = bf16[2048,7168]{1,0:T(8,128)(2,1)S(1)} custom-call(bf16[2048,7168]{1,0:T(8,128)(2,1)} %x_ref.1, bf16[7168,640]{1,0:T(8,128)(2,1)} %wg_ref.1, bf16[7168,640]{1,0:T(8,128)(2,1)} %wu_ref.1, bf16[640,7168]{1,0:T(8,128)(2,1)} %wd_ref.1), custom_call_target="tpu_custom_call" | custom-call | tf_op jit(solution)/shard_map/mlp_all_reduce/pallas_call | solution.py:558
  232.8 9.8 %store.1 = bf16[2048,7168]{1,0:T(8,128)(2,1)} custom-call(bf16[2048,7168]{1,0:T(8,128)(2,1)S(1)} %mlp_all_reduce.1.y_ref), custom_call_target="tpu_custom_call" | custom-call | tf_op jit(solution)/shard_map/store/pallas_call | solution.py:616

commit v3 on v2

--- a/solution.py
+++ b/solution.py
@@ -40,11 +40,15 @@
 GSEND = 6
 
 
+def k_block(rows, F):
+    return (rows - F) // 256 * 256
+
+
 def split(W):
-    return W * 5 // 7 // 128 * 128 if W > 256 else W // 2
-
-
-def kernel(R, x_ref, wg_ref, wu_ref, wd_ref, y_ref, xbuf, hidden, term, acco, acci, pairsend, pairrecv,
+    return W * 6 // 7 // 128 * 128 if W > 256 else W // 2
+
+
+def kernel(R, x_ref, wg_ref, wu_ref, wd_ref, y_ref, wrest, xbuf, hidden, term, acco, acci, pairsend, pairrecv,
            xsend, xrecv, z1send, z1recv, z2send, z2recv, z3send, z3recv, ysend, yrecv, fin,
            accco, accci, c1send, c1recv, c2send, c2recv, c3send, c3recv, c4send, c4recv,
            w_sem, x_sem, sp, rp, sx, rx, sz1, rz1, sz2, rz2, sz3, rz3, sy, ry,
@@ -58,10 +62,10 @@
     Q = R // 2
     G = Q // PIECES
     NG = N * PIECES
-    KB = y_ref.shape[0] - F
+    KB = k_block(y_ref.shape[0], F)
     NB = D // KB
     REST = D - NB * KB
-    assert 2 * REST <= KB and NB * 2 * F + F <= D
+    assert NB * 2 * F <= D
 
     me = lax.axis_index("tp")
     c = lax.rem(me, 2)
@@ -96,7 +100,7 @@
                 dst = y_ref.at[pl.ds(F, KB), pl.ds((2 * b + i) * F, F)]
                 src = ref.at[pl.ds(b * KB, KB)]
             else:
-                dst = y_ref.at[pl.ds(F + i * REST, REST), pl.ds(NB * 2 * F, F)]
+                dst = wrest.at[:, pl.ds(i * F, F)]
                 src = ref.at[pl.ds(NB * KB, REST)]
             copies.append(pltpu.make_async_copy(src, dst, w_sem.at[b, i]))
         return copies
@@ -221,22 +225,10 @@
                 for copy in weight_copies(b):
                     copy.wait()
 
-            if b < NB:
-                part = jnp.dot(
-                    xbuf[xs, :, b * KB:(b + 1) * KB],
-                    y_ref[F:F + KB, b * 2 * F:(b + 1) * 2 * F],
-                    preferred_element_type=F32,
-                )
-                h = part if h is None else h + part
-        gate, up = (
-            h[:, i * F:(i + 1) * F] + jnp.dot(
-                xbuf[xs, :, NB * KB:],
-                y_ref[F + i * REST:F + (i + 1) * REST, NB * 2 * F:NB * 2 * F + F],
-                preferred_element_type=F32,
-            )
-            for i in range(2)
-        )
-        hidden[...] = (jax.nn.silu(gate) * up).astype(BF16)
+            rows = y_ref[F:F + KB, b * 2 * F:(b + 1) * 2 * F] if b < NB else wrest[...]
+            part = jnp.dot(xbuf[xs, :, b * KB:min(D, (b + 1) * KB)], rows, preferred_element_type=F32)
+            h = part if h is None else h + part
+        hidden[...] = (jax.nn.silu(h[:, :F]) * h[:, F:]).astype(BF16)
 
     def s0(k):
         @pl.when(k == 0)
@@ -554,13 +546,15 @@
         W3 = W - W1
         any_spec = pl.BlockSpec(memory_space=pl.ANY)
         dma = lambda *shape: pltpu.SemaphoreType.DMA(shape)
-        blocks = D // (rows - F) + 2
+        kb = k_block(rows, F)
+        blocks = D // kb + 2
         y = pl.pallas_call(
             functools.partial(kernel, R),
             out_shape=pltpu.VMEM((rows, D), BF16),
             in_specs=[any_spec] * 4,
             out_specs=pl.BlockSpec(memory_space=pltpu.VMEM),
             scratch_shapes=[
+                pltpu.VMEM((D % kb, 2 * F), BF16),
                 pltpu.VMEM((2, R, D), BF16),
                 pltpu.VMEM((R, F), BF16),
                 pltpu.VMEM((KT, 2, 2, R, W), F32),

time: 243 us -> 241 us (level)
  no operation moved by 1% of the time
where the time goes in v3:
time: 241 us
  Pallas kernels  241 us (100%)
    pallas_call x1, Pallas kernels, step(): pl.pallas_call(functools.partial(kernel, R), out_shape=pltpu.VMEM((rows,...  231 us
    pallas_call x1, Pallas kernels, step(): pl.pallas_call(store_kernel, out_shape=jax.ShapeDtypeStruct((rows, D), BF...  9.84 us

profile of v3, /device:TPU:1, one launch (start us, length us, event | category | flops | bytes accessed | tf_op | source)
XLA Modules:
  0.0 240.9 jit_solution(10332454044251772271)
XLA Ops:
  0.0 231.1 %mlp_all_reduce.1.y_ref = bf16[2048,7168]{1,0:T(8,128)(2,1)S(1)} custom-call(bf16[2048,7168]{1,0:T(8,128)(2,1)} %x_ref.1, bf16[7168,640]{1,0:T(8,128)(2,1)} %wg_ref.1, bf16[7168,640]{1,0:T(8,128)(2,1)} %wu_ref.1, bf16[640,7168]{1,0:T(8,128)(2,1)} %wd_ref.1), custom_call_target="tpu_custom_call" | custom-call | tf_op jit(solution)/shard_map/mlp_all_reduce/pallas_call | solution.py:551
  231.1 9.8 %store.1 = bf16[2048,7168]{1,0:T(8,128)(2,1)} custom-call(bf16[2048,7168]{1,0:T(8,128)(2,1)S(1)} %mlp_all_reduce.1.y_ref), custom_call_target="tpu_custom_call" | custom-call | tf_op jit(solution)/shard_map/store/pallas_call | solution.py:610
